TPU v7x, 1024 devices: a whole 8x8x8 slice. The times are simulated.
1024 devices in a mesh: tile: 64 (over z, x), conv: 16 (over y, core).
Axes of the slice: x: 8, y: 8, z: 8, core: 2. Of those that a mesh axis runs over, the one named last changes fastest.
Arguments:
- field: float32 [256, 786432], P(None, ('tile', 'conv')), may hold values from -6 to 6
- interp: bfloat16 [1048576, 384], P(('tile', 'conv')), may hold values from -0.1875 to 0.1875
- conv_blocks: bfloat16 [2048, 3, 256, 256], P(('tile', 'conv')), may hold values from -0.21875 to 0.21875
- band_shift: int32 [2048, 3], P(('tile', 'conv')), may hold values from 0 to 1
- owner: int32 [393216, 1], P(('tile', 'conv')), may hold values from 0 to 15; in each aligned block of 384 rows (0 to 383, 384 to 767, ...) at most 32 rows name the same one
- edge_index: int32 [2048, 128], P(('tile', 'conv')), may hold values from 0 to 767, as said below
Outputs:
- correlated: float32 [256, 786432], P(None, ('tile', 'conv'))
Inputs may be any that keep to these rules, and one draw needn't show every extreme that they name: `edge_index`: row 2b lists the first 128 columns of domain b in some order, row 2b + 1 its last 128 columns in some order. Among the 384 points of one domain no owner is named more than 32 times, and in some domains one owner is named exactly 32 times.
All inputs are finite; a program needn't handle non-finite values.
Results may differ from a plain program's by a relative error of at most 0.0049.
Values may be sent and summed in bfloat16 or wider, within the bound.
A program may use at most 32 MiB of HBM per device.

v0:
```python
import jax
import jax.numpy as jnp
from jax import lax
from jax.sharding import PartitionSpec as P


def padded(cells, sides, width):
    for axis, dim in sides:
        count = lax.axis_size(axis)
        head = lax.slice_in_dim(cells, 0, width, axis=dim)
        tail = lax.slice_in_dim(cells, cells.shape[dim] - width, cells.shape[dim], axis=dim)
        cells = jnp.concatenate(
            [
                lax.ppermute(tail, axis, [(i, (i + 1) % count) for i in range(count)]),
                cells,
                lax.ppermute(head, axis, [((i + 1) % count, i) for i in range(count)]),
            ],
            axis=dim,
        )
    return cells


def with_halo(x, sides, width):
    edges = {}
    for axis, dim in sides:
        size, length = (lax.axis_size(axis), x.shape[dim])
        up = [(i, (i + 1) % size) for i in range(size)]
        last = lax.slice_in_dim(x, length - width, length, axis=dim)
        leading = lax.slice_in_dim(x, 0, width, axis=dim)
        edges[dim] = (
            lax.ppermute(last, axis, up),
            lax.ppermute(leading, axis, [(b, a) for a, b in up]),
        )
    done = []
    for _, dim in sides:
        low, high = edges[dim]
        around = [(width, width) if d in done else (0, 0) for d in range(x.ndim)]
        x = jnp.concatenate([jnp.pad(low, around), x, jnp.pad(high, around)], axis=dim)
        done.append(dim)
    return x


def contract_last(left_side, right_side):
    return lax.dot_general(
        left_side, right_side, (((1,), (1,)), ((), ())), preferred_element_type=jnp.float32
    )


def convolve(values, conv_blocks, band_shift):
    height = values.shape[0]
    owned_blocks = conv_blocks.shape[0]
    points = conv_blocks.shape[2]
    pieces = values.reshape(height, owned_blocks, points)
    source = (jnp.arange(owned_blocks, dtype=jnp.int32)[:, None] + band_shift) % owned_blocks
    select = (
        source[:, :, None] == jnp.arange(owned_blocks, dtype=jnp.int32)[None, None, :]
    ).astype(jnp.bfloat16)
    picked = jnp.einsum("rsp,jbs->rjbp", pieces, select, preferred_element_type=jnp.float32).astype(
        jnp.bfloat16
    )
    forward = jnp.einsum(
        "rjbp,jbpq->rjq", picked, conv_blocks, preferred_element_type=jnp.float32
    ).astype(jnp.bfloat16)
    backward = jnp.einsum(
        "rjq,jbpq->rjbp", forward, conv_blocks, preferred_element_type=jnp.float32
    )
    adjoint = jnp.einsum(
        "rjbp,jbs->rsp", backward, select.astype(jnp.float32), precision=lax.Precision.HIGHEST
    )
    return adjoint.reshape(height, owned_blocks * points).astype(jnp.bfloat16)


def on_device(field, interp, conv_blocks, band_shift, owner, edge_index):
    columns = field.shape[1]
    rim_width = edge_index.shape[1]
    groups = lax.axis_size("conv")
    slot_count = conv_blocks.shape[0] * conv_blocks.shape[2]
    capacity = slot_count // groups
    rounded = field.astype(jnp.bfloat16)
    left_list = edge_index[0]
    right_list = edge_index[1]
    rim_values = jnp.concatenate(
        [jnp.take(rounded, left_list, axis=1), jnp.take(rounded, right_list, axis=1)], axis=1
    )
    interior = jnp.dot(
        rounded, interp[rim_width : rim_width + columns], preferred_element_type=jnp.float32
    )
    widened = padded(rim_values, ((("tile", "conv"), 1),), rim_width)
    from_left = widened[:, :rim_width]
    from_right = widened[:, 3 * rim_width :]
    subgrid = interior + jnp.dot(from_left, interp[:rim_width], preferred_element_type=jnp.float32)
    subgrid = subgrid + jnp.dot(
        from_right, interp[rim_width + columns :], preferred_element_type=jnp.float32
    )
    subgrid = subgrid.astype(jnp.bfloat16)
    owners = owner[:, 0]
    choose = (owners[:, None] == jnp.arange(groups, dtype=jnp.int32)[None, :]).astype(jnp.int32)
    before = jnp.cumsum(choose, axis=0) - choose
    position = jnp.sum(before * choose, axis=1)
    slot_index = owners * capacity + position
    placement = (slot_index[:, None] == jnp.arange(slot_count, dtype=jnp.int32)[None, :]).astype(
        jnp.bfloat16
    )
    outgoing = jnp.dot(subgrid, placement, preferred_element_type=jnp.float32).astype(jnp.bfloat16)
    incoming = lax.all_to_all(
        convolve(
            lax.all_to_all(outgoing, "conv", split_axis=1, concat_axis=1, tiled=True),
            conv_blocks,
            band_shift,
        ),
        "conv",
        split_axis=1,
        concat_axis=1,
        tiled=True,
    )
    returned = contract_last(incoming, placement).astype(jnp.bfloat16)
    left_part = jnp.dot(returned, interp[:rim_width].T, preferred_element_type=jnp.float32)
    right_part = jnp.dot(
        returned, interp[rim_width + columns :].T, preferred_element_type=jnp.float32
    )
    edge_sums = with_halo(
        jnp.concatenate([left_part, right_part], axis=1).astype(jnp.bfloat16),
        ((("tile", "conv"), 1),),
        rim_width,
    ).astype(jnp.float32)
    interior_part = jnp.dot(
        returned, interp[rim_width : rim_width + columns].T, preferred_element_type=jnp.float32
    )
    result = interior_part.at[:, left_list].add(edge_sums[:, :rim_width])
    result = result.at[:, right_list].add(edge_sums[:, 3 * rim_width :])
    return result


def solution(mesh):
    return jax.shard_map(
        on_device,
        mesh=mesh,
        in_specs=(
            P(None, ("tile", "conv")),
            P(("tile", "conv"), None),
            P(("tile", "conv"), None, None, None),
            P(("tile", "conv"), None),
            P(("tile", "conv"), None),
            P(("tile", "conv"), None),
        ),
        out_specs=P(None, ("tile", "conv")),
        check_vma=False,
    )
```

profile of v0, /device:TPU:1, one launch (start us, length us, event | category | flops | bytes accessed | tf_op | source)
XLA Modules:
  0.0 81.4 jit_solution(12336913850897446305)
XLA Ops:
  0.0 0.0 copy-start
  0.0 0.0 copy-start.1
  0.0 0.8 %compare_and_fusion = (pred[128]{0:T(512)(128)(4,1)S(1)}, s32[128]{0:T(128)S(1)}, pred[128]{0:T(512)(128)(4,1)S(1)}, s32[128]{0:T(128)S(1)}) fusion(s32[2,128]{1,0:T(2,128)} %param.13), kind=kLoop, calls=%fused_computation.73 | loop fusion | flops 1536 | bytes 2304 | tf_op jit(solution)/shard_map/jit(_take)/and | solution.py:83
  0.8 1.3 %copy.10 = bf16[256,768]{0,1:T(8,128)(2,1)S(1)} copy(f32[256,768]{1,0:T(8,128)} %param.8) | data formatting | bytes 1179648 | tf_op args[0]
  2.1 0.0 copy-start.3
  2.2 0.8 %gather_fusion = bf16[128,256]{1,0:T(8,128)(2,1)S(1)} fusion(bf16[256,768]{0,1:T(8,128)(2,1)S(1)} %copy.10, s32[1024]{0:T(1024)S(1)} %pad_clamp_fusion.1), kind=kCustom, calls=%fused_computation.clone | custom fusion | bytes 131584 | tf_op jit(solution)/shard_map/jit(_take)/gather | solution.py:83
  3.0 0.1 select_bitcast_fusion.1
  3.1 4.7 %collective-permute-start = (bf16[256,128]{0,1:T(8,128)(2,1)S(1)}, bf16[256,128]{0,1:T(8,128)(2,1)S(1)}, u32[]{:S(2)}, u32[]{:S(2)}) collective-permute-start(bf16[256,128]{0,1:T(8,128)(2,1)S(1)} %select_bitcast_fusion.1), channel_id=1, source_target_pairs={{0,1},{1,2},{2,3},{3,4},{4,5},{5,6},{6,7},{7,8},{8,9},{9,10},{10,1... | collective-permute-start | bytes 196616 | tf_op jit(solution)/shard_map/ppermute | solution.py:14
  7.8 0.8 %gather_fusion.1 = bf16[128,256]{1,0:T(8,128)(2,1)S(1)} fusion(bf16[256,768]{0,1:T(8,128)(2,1)S(1)} %copy.10, s32[1024]{0:T(1024)S(1)} %pad_clamp_fusion), kind=kCustom, calls=%fused_computation.1.clone | custom fusion | bytes 131584 | tf_op jit(solution)/shard_map/jit(_take)/gather | solution.py:83
  8.7 0.1 select_bitcast_fusion
  8.8 13.2 %collective-permute-start.1 = (bf16[256,128]{0,1:T(8,128)(2,1)S(1)}, bf16[256,128]{0,1:T(8,128)(2,1)S(1)}, u32[]{:S(2)}, u32[]{:S(2)}) collective-permute-start(bf16[256,128]{0,1:T(8,128)(2,1)S(1)} %select_bitcast_fusion), channel_id=1, source_target_pairs={{1,0},{2,1},{3,2},{4,3},{5,4},{6,5},{7,6},{8,7},{9,8},{10,9},{11,1... | collective-permute-start | bytes 196616 | tf_op jit(solution)/shard_map/ppermute | solution.py:16
  22.0 0.0 copy-done.1
  22.0 0.4 fusion.22
  22.4 0.0 copy-done.3
  22.4 0.0 copy-start.5
  22.5 0.9 %reduce-window.6 = s32[16,3,128]{2,0,1:T(8,128)S(1)} reduce-window(s32[16,3,128]{2,0,1:T(8,128)S(1)} %fusion.46, s32[]{:T(128)} %constant.30.clone.1), window={size=1x1x128 pad=0_0x0_0x127_0}, to_apply=%region_0.0 | reduce-window | flops 780288 | bytes 49156 | tf_op jit(solution)/shard_map/reduce-window
  23.3 0.2 slice_reduce_fusion
  23.6 0.1 fusion.45
  23.7 0.0 collective-permute-done
  23.7 0.2 convolution_add_fusion.1
  24.0 0.0 collective-permute-done.1
  24.0 0.5 convolution_convert_fusion
  24.5 0.8 %copy.12 = bf16[256,512]{0,1:T(8,128)(2,1)} copy(bf16[256,512]{1,0:T(8,128)(2,1)S(1)} %convolution_convert_fusion) | data formatting | bytes 524288 | tf_op jit(solution)/shard_map/convert_element_type | solution.py:104
  25.3 11.6 %all-to-all-start = ((bf16[256,16,32]{0,2,1:T(8,128)(2,1)}), bf16[256,16,32]{0,2,1:T(8,128)(2,1)S(1)}, u32[]{:S(2)}, u32[]{:S(2)}) async-start(bf16[256,16,32]{0,2,1:T(8,128)(2,1)} %bitcast.7), calls=%async_computation | async-start | bytes 524288 | tf_op jit(solution)/shard_map/all_to_all | solution.py:107
  36.8 0.0 copy-done.5
  36.9 11.7 %all-to-all-done = bf16[256,16,32]{0,2,1:T(8,128)(2,1)S(1)} async-done(((bf16[256,16,32]{0,2,1:T(8,128)(2,1)}), bf16[256,16,32]{0,2,1:T(8,128)(2,1)S(1)}, u32[]{:S(2)}, u32[]{:S(2)}) %all-to-all-start) | async-done | bytes 262176 | tf_op jit(solution)/shard_map/all_to_all | solution.py:107
  48.6 0.2 copy.17
  48.8 1.0 %fusion.47 = bf16[2,3,256,256]{3,1,2,0:T(4,128)(2,1)S(1)} fusion(bf16[256,2,256,1]{2,1,0,3:T(2,128)(2,1)S(1)} %copy.17, s32[2,3]{1,0:T(2,128)S(1)} %and_select_fusion), kind=kOutput, calls=%fused_computation.63 | convolution fusion | flops 1572876 | bytes 1048600 | tf_op jit(solution)/shard_map/rsp,jbs->rjbp/dot_general | solution.py:58
  49.8 0.0 copy-done
  49.8 0.7 fusion.18
  50.5 0.0 copy-start.4
  50.5 0.0 copy-start.2
  50.5 2.9 %fusion.11 = bf16[256,2,256]{2,1,0:T(2,128)(2,1)S(1)} fusion(f32[2,256,3,256]{3,1,2,0:T(8,128)S(1)} %fusion.18, s32[2,3]{1,0:T(2,128)S(1)} %and_select_fusion), kind=kOutput, calls=%fused_computation.17 | convolution fusion | flops 9568268 | bytes 1835032 | tf_op jit(solution)/shard_map/rjbp,jbs->rsp/dot_general | solution.py:67
  53.4 0.9 %copy.13 = bf16[256,2,256]{0,2,1:T(8,128)(2,1)} copy(bf16[256,2,256]{2,1,0:T(2,128)(2,1)S(1)} %fusion.11) | data formatting | bytes 524288 | tf_op jit(solution)/shard_map/convert_element_type | solution.py:70
  54.3 3.4 %all-to-all-start.1 = ((bf16[256,16,32]{0,2,1:T(8,128)(2,1)}), bf16[256,16,32]{0,2,1:T(8,128)(2,1)S(1)}, u32[]{:S(2)}, u32[]{:S(2)}) async-start(bf16[256,16,32]{0,2,1:T(8,128)(2,1)} %bitcast.20), calls=%async_computation.1 | async-start | bytes 524288 | tf_op jit(solution)/shard_map/all_to_all | solution.py:105
  57.7 0.0 copy-done.4
  57.8 10.9 %all-to-all-done.1 = bf16[256,16,32]{0,2,1:T(8,128)(2,1)S(1)} async-done(((bf16[256,16,32]{0,2,1:T(8,128)(2,1)}), bf16[256,16,32]{0,2,1:T(8,128)(2,1)S(1)}, u32[]{:S(2)}, u32[]{:S(2)}) %all-to-all-start.1) | async-done | bytes 262176 | tf_op jit(solution)/shard_map/all_to_all | solution.py:105
  68.6 0.4 convolution_convert_fusion.1
  69.1 0.0 copy-done.2
  69.1 0.2 convolution_convert_fusion.3
  69.3 0.2 convolution_convert_fusion.2
  69.5 1.9 %collective-permute-start.2 = (bf16[256,128]{0,1:T(8,128)(2,1)S(1)}, bf16[256,128]{0,1:T(8,128)(2,1)S(1)}, u32[]{:S(2)}, u32[]{:S(2)}) collective-permute-start(bf16[256,128]{0,1:T(8,128)(2,1)S(1)} %convolution_convert_fusion.3), channel_id=1, source_target_pairs={{0,1},{1,2},{2,3},{3,4},{4,5},{5,6},{6,7},{7,8},{8,9},{9,10},{10,1... | collective-permute-start | bytes 196616 | tf_op jit(solution)/shard_map/ppermute | solution.py:31
  71.5 2.4 %collective-permute-start.3 = (bf16[256,128]{0,1:T(8,128)(2,1)S(1)}, bf16[256,128]{0,1:T(8,128)(2,1)S(1)}, u32[]{:S(2)}, u32[]{:S(2)}) collective-permute-start(bf16[256,128]{0,1:T(8,128)(2,1)S(1)} %convolution_convert_fusion.2), channel_id=1, source_target_pairs={{1,0},{2,1},{3,2},{4,3},{5,4},{6,5},{7,6},{8,7},{9,8},{10,9},{11,1... | collective-permute-start | bytes 196616 | tf_op jit(solution)/shard_map/ppermute | solution.py:32
  73.9 0.4 fusion.20
  74.3 0.0 collective-permute-done.2
  74.3 2.8 %collective-permute-done.3 = bf16[256,128]{0,1:T(8,128)(2,1)S(1)} collective-permute-done((bf16[256,128]{0,1:T(8,128)(2,1)S(1)}, bf16[256,128]{0,1:T(8,128)(2,1)S(1)}, u32[]{:S(2)}, u32[]{:S(2)}) %collective-permute-start.3) | collective-permute-done | bytes 65568 | tf_op jit(solution)/shard_map/ppermute | solution.py:32
  77.1 1.6 %scatter_custom_fusion = f32[256,768]{0,1:T(8,128)S(1)} fusion(f32[256,768]{0,1:T(8,128)S(1)} %fusion.20, s32[128]{0:T(128)S(1)} %get-tuple-element.11, bf16[256,128]{0,1:T(8,128)(2,1)S(1)} %collective-permute-done.3, bf16[]{:T(256)} %constant.44, bf16[256,128]{0,1:T(8,128)(2,1)S(1)} %convolution_convert_fusion.3, ...), kind=kCustom, calls=%fused_computation.31 | custom fusion | flops 294912 | bytes 1048578 | tf_op jit(solution)/shard_map/scatter-add | solution.py:129
  78.7 1.6 %scatter_custom_fusion.1 = f32[256,768]{0,1:T(8,128)S(1)} fusion(f32[256,768]{0,1:T(8,128)S(1)} %scatter_custom_fusion, s32[128]{0:T(128)S(1)} %get-tuple-element.10, bf16[256,128]{0,1:T(8,128)(2,1)S(1)} %collective-permute-done.3, bf16[]{:T(256)} %constant.44, bf16[256,128]{0,1:T(8,128)(2,1)S(1)} %convolution_convert_fusion.3, ...), kind=kCustom, calls=%fused_computation.32 | custom fusion | flops 294912 | bytes 1048578 | tf_op jit(solution)/shard_map/scatter-add | solution.py:130
  80.3 1.1 %copy.15 = f32[256,768]{1,0:T(8,128)} copy(f32[256,768]{0,1:T(8,128)S(1)} %scatter_custom_fusion.1) | data formatting | bytes 1572864 | tf_op jit(solution)/shard_map/scatter-add | solution.py:130
  (8 shorter events, 0.1 us)
Async XLA Ops:
  0.0 49.8 %copy-start = (bf16[2,3,256,256]{3,2,1,0:T(8,128)(2,1)S(1)}, bf16[2,3,256,256]{3,2,1,0:T(8,128)(2,1)}, u32[]{:S(2)}) copy-start(bf16[2,3,256,256]{3,2,1,0:T(8,128)(2,1)} %param.10) | copy-start | bytes 2359300
  0.0 22.0 %copy-start.1 = (bf16[1024,384]{1,0:T(8,128)(2,1)S(1)}, bf16[1024,384]{1,0:T(8,128)(2,1)}, u32[]{:S(2)}) copy-start(bf16[1024,384]{1,0:T(8,128)(2,1)} %param.9) | copy-start | bytes 2359300
  2.1 20.3 %copy-start.3 = (s32[384,1]{0,1:T(1,128)S(1)}, s32[384,1]{0,1:T(1,128)}, u32[]{:S(2)}) copy-start(s32[384,1]{0,1:T(1,128)} %param.12) | copy-start | bytes 4612
  3.1 20.6 %collective-permute-start = (bf16[256,128]{0,1:T(8,128)(2,1)S(1)}, bf16[256,128]{0,1:T(8,128)(2,1)S(1)}, u32[]{:S(2)}, u32[]{:S(2)}) collective-permute-start(bf16[256,128]{0,1:T(8,128)(2,1)S(1)} %select_bitcast_fusion.1), channel_id=1, source_target_pairs={{0,1},{1,2},{2,3},{3,4},{4,5},{5,6},{6,7},{7,8},{8,9},{9,10},{10,1... | collective-permute-start | bytes 196616 | tf_op jit(solution)/shard_map/ppermute | solution.py:14
  8.8 15.2 %collective-permute-start.1 = (bf16[256,128]{0,1:T(8,128)(2,1)S(1)}, bf16[256,128]{0,1:T(8,128)(2,1)S(1)}, u32[]{:S(2)}, u32[]{:S(2)}) collective-permute-start(bf16[256,128]{0,1:T(8,128)(2,1)S(1)} %select_bitcast_fusion), channel_id=1, source_target_pairs={{1,0},{2,1},{3,2},{4,3},{5,4},{6,5},{7,6},{8,7},{9,8},{10,9},{11,1... | collective-permute-start | bytes 196616 | tf_op jit(solution)/shard_map/ppermute | solution.py:16
  22.4 14.4 %copy-start.5 = (s32[2,3]{1,0:T(2,128)S(1)}, s32[2,3]{1,0:T(2,128)}, u32[]{:S(2)}) copy-start(s32[2,3]{1,0:T(2,128)} %param.11) | copy-start | bytes 76
  25.3 23.3 %all-to-all-start = ((bf16[256,16,32]{0,2,1:T(8,128)(2,1)}), bf16[256,16,32]{0,2,1:T(8,128)(2,1)S(1)}, u32[]{:S(2)}, u32[]{:S(2)}) async-start(bf16[256,16,32]{0,2,1:T(8,128)(2,1)} %bitcast.7), calls=%async_computation | async-start | bytes 524288 | tf_op jit(solution)/shard_map/all_to_all | solution.py:107
  50.5 7.3 %copy-start.4 = (s32[2,128]{1,0:T(2,128)S(1)}, s32[2,128]{1,0:T(2,128)}, u32[]{:S(2)}) copy-start(s32[2,128]{1,0:T(2,128)} %param.13) | copy-start | bytes 3076
  50.5 18.6 %copy-start.2 = (bf16[1024,384]{1,0:T(8,128)(2,1)S(1)}, bf16[1024,384]{1,0:T(8,128)(2,1)}, u32[]{:S(2)}) copy-start(bf16[1024,384]{1,0:T(8,128)(2,1)} %param.9) | copy-start | bytes 2359300
  54.3 14.3 %all-to-all-start.1 = ((bf16[256,16,32]{0,2,1:T(8,128)(2,1)}), bf16[256,16,32]{0,2,1:T(8,128)(2,1)S(1)}, u32[]{:S(2)}, u32[]{:S(2)}) async-start(bf16[256,16,32]{0,2,1:T(8,128)(2,1)} %bitcast.20), calls=%async_computation.1 | async-start | bytes 524288 | tf_op jit(solution)/shard_map/all_to_all | solution.py:105
  69.5 4.7 %collective-permute-start.2 = (bf16[256,128]{0,1:T(8,128)(2,1)S(1)}, bf16[256,128]{0,1:T(8,128)(2,1)S(1)}, u32[]{:S(2)}, u32[]{:S(2)}) collective-permute-start(bf16[256,128]{0,1:T(8,128)(2,1)S(1)} %convolution_convert_fusion.3), channel_id=1, source_target_pairs={{0,1},{1,2},{2,3},{3,4},{4,5},{5,6},{6,7},{7,8},{8,9},{9,10},{10,1... | collective-permute-start | bytes 196616 | tf_op jit(solution)/shard_map/ppermute | solution.py:31
  71.5 5.6 %collective-permute-start.3 = (bf16[256,128]{0,1:T(8,128)(2,1)S(1)}, bf16[256,128]{0,1:T(8,128)(2,1)S(1)}, u32[]{:S(2)}, u32[]{:S(2)}) collective-permute-start(bf16[256,128]{0,1:T(8,128)(2,1)S(1)} %convolution_convert_fusion.2), channel_id=1, source_target_pairs={{1,0},{2,1},{3,2},{4,3},{5,4},{6,5},{7,6},{8,7},{9,8},{10,9},{11,1... | collective-permute-start | bytes 196616 | tf_op jit(solution)/shard_map/ppermute | solution.py:32
where the time goes:
time: 81.9 us; the launch traced here: 81.4 us
  starting transfers between devices  37.3 us (46%)
  waiting for transfers between devices  25.4 us (31%)
  matrix products  6.94 us (8%)
  local copies, waits for them, and re-layouts  6.3 us (8%)
  other arithmetic  5.27 us (6%)
    ppermute x1, starting transfers between devices, padded(): lax.ppermute(head, axis, [((i + 1) % count, i) for i in range(count)])  13.2 us
    all_to_all x1, waiting for transfers between devices, on_device(): lax.all_to_all(outgoing, 'conv', split_axis=1, concat_axis=1, tiled=True)  11.7 us
    all_to_all x1, starting transfers between devices, on_device(): lax.all_to_all(outgoing, 'conv', split_axis=1, concat_axis=1, tiled=True)  11.6 us
    all_to_all x1, waiting for transfers between devices, on_device(): lax.all_to_all(convolve(lax.all_to_all(outgoing, 'conv', split_axis=1, co...  10.9 us
    ppermute x1, starting transfers between devices, padded(): lax.ppermute(tail, axis, [(i, (i + 1) % count) for i in range(count)])  4.7 us
    all_to_all x1, starting transfers between devices, on_device(): lax.all_to_all(convolve(lax.all_to_all(outgoing, 'conv', split_axis=1, co...  3.43 us
    dot_general x1, matrix products, convolve(): jnp.einsum('rjbp,jbs->rsp', backward, select.astype(jnp.float32), precisi...  2.94 us
    ppermute x1, waiting for transfers between devices, with_halo(): lax.ppermute(leading, axis, [(b, a) for a, b in up])  2.76 us
  transfers between devices with their start and end apart: 6, of which 3 were waited for; matrix products, arithmetic and copies ran while one was open for 4% of the time, Pallas kernels for 0%

commit v1 on v0

v1 whole, which is shorter than its diff:
```python
import jax
import jax.numpy as jnp
from jax import lax
from jax.experimental import pallas as pl
from jax.experimental.pallas import tpu as pltpu
from jax.sharding import PartitionSpec as P

MESH = pl.DeviceIdType.MESH
F32 = jnp.float32
BF16 = jnp.bfloat16
NT = (((1,), (1,)), ((), ()))
NN = (((1,), (0,)), ((), ()))


def mm(a, b, dims=NN):
    return lax.dot_general(a, b, dims, preferred_element_type=F32)


def make_kernel(n_tile, n_conv, rows, columns, rim, points, blocks, bands, block_points):
    slots = blocks * block_points
    cap = slots // n_conv
    per_block = block_points // cap
    half = 128
    halves = rows // half
    offsets = sorted(range(1, n_conv), key=lambda d: (-min(d, n_conv - d), d))

    def kernel(
        field, interp, conv, shift, owner, edges, out,
        xf, ib, wb, sh, ow, eg, rims, halo, pt, qt, xb, mid, out_t, g_t0, g_t1, adj_t, inc_t, edge_out, edge_in, wt,
        load_sem, halo_send, halo_recv, go_send, go_recv, back_send, back_recv, edge_send, edge_recv,
    ):
        tile = lax.axis_index("tile")
        me = lax.axis_index("conv")
        index = tile * n_conv + me
        total = n_tile * n_conv
        right = lax.rem(index + 1, total)
        left = lax.rem(index + total - 1, total)
        right_id = (right // n_conv, lax.rem(right, n_conv))
        left_id = (left // n_conv, lax.rem(left, n_conv))

        def peer(d):
            return (tile, lax.rem(me + d, n_conv))

        barrier = pltpu.get_barrier_semaphore()
        for target in [left_id, right_id] + [peer(d) for d in offsets]:
            pl.semaphore_signal(barrier, inc=1, device_id=target, device_id_type=MESH)

        loads = [
            pltpu.make_async_copy(edges, eg, load_sem.at[0]),
            pltpu.make_async_copy(field.at[:, pl.ds(columns - rim, rim)], xf.at[:, pl.ds(columns - rim, rim)], load_sem.at[1]),
            pltpu.make_async_copy(field.at[:, pl.ds(0, rim)], xf.at[:, pl.ds(0, rim)], load_sem.at[2]),
            pltpu.make_async_copy(owner, ow, load_sem.at[3]),
            pltpu.make_async_copy(interp, ib, load_sem.at[4]),
            pltpu.make_async_copy(
                field.at[:, pl.ds(rim, columns - 2 * rim)], xf.at[:, pl.ds(rim, columns - 2 * rim)], load_sem.at[5]
            ),
            pltpu.make_async_copy(conv, wb, load_sem.at[6]),
            pltpu.make_async_copy(shift, sh, load_sem.at[7]),
        ]
        for load in loads:
            load.start()

        for i in range(3):
            loads[i].wait()
        down = lax.broadcasted_iota(jnp.int32, (rim, rim), 0)
        pick_left = (down == eg[0:1, :]).astype(F32).astype(BF16)
        pick_right = (down + (columns - rim) == eg[1:2, :]).astype(F32).astype(BF16)
        edge_cols = (slice(columns - rim, columns), slice(0, rim))
        for side, pick in ((0, pick_right), (1, pick_left)):
            cells = xf[:, edge_cols[side]].astype(BF16)
            xb[:, edge_cols[side]] = cells
            rims[side] = mm(cells, pick).astype(BF16).reshape(halves, half, rim)

        pl.semaphore_wait(barrier, n_conv + 1)

        halo_copies = []
        for h in range(halves):
            for side, target in ((0, right_id), (1, left_id)):
                copy = pltpu.make_async_remote_copy(
                    src_ref=rims.at[side, h], dst_ref=halo.at[side, h],
                    send_sem=halo_send.at[side, h], recv_sem=halo_recv.at[side, h],
                    device_id=target, device_id_type=MESH,
                )
                copy.start()
                halo_copies.append(copy)

        loads[3].wait()
        owners = ow[...]
        named = (lax.broadcasted_iota(jnp.int32, (n_conv, points), 0) == owners).astype(F32)
        earlier = (
            lax.broadcasted_iota(jnp.int32, (points, points), 0) < lax.broadcasted_iota(jnp.int32, (points, points), 1)
        ).astype(F32).astype(BF16)
        before = mm(named.astype(BF16), earlier)
        rank = jnp.sum(before * named, axis=0, keepdims=True)
        slot = owners.astype(F32) * cap + rank
        pt[...] = (lax.broadcasted_iota(jnp.int32, (slots, points), 0).astype(F32) == slot).astype(F32).astype(BF16)
        loads[4].wait()
        extended = columns + 2 * rim
        for start in range(0, extended, 256):
            qt[:, start:start + 256] = mm(pt[...], ib[start:start + 256, :], NT).astype(BF16)
        loads[5].wait()
        xb[:, rim:columns - rim] = xf[:, rim:columns - rim].astype(BF16)
        for h in range(halves):
            mid[h] = mm(qt[:, rim:rim + columns], xb[h * half:(h + 1) * half, :], NT)

        g_t = (g_t0, g_t1)
        inc = (inc_t.at[0], inc_t.at[1])

        def exchange(h, src, dst, send, recv):
            copies = []
            for d in offsets:
                to = lax.rem(me + d, n_conv)
                copy = pltpu.make_async_remote_copy(
                    src_ref=src.at[h, to // per_block, pl.ds(pl.multiple_of(lax.rem(to, per_block) * cap, cap), cap)],
                    dst_ref=dst.at[me // per_block, pl.ds(pl.multiple_of(lax.rem(me, per_block) * cap, cap), cap)],
                    send_sem=send.at[h, d], recv_sem=recv.at[h, d],
                    device_id=peer(d), device_id_type=MESH,
                )
                copy.start()
                copies.append(copy)
            mine = pl.ds(pl.multiple_of(lax.rem(me, per_block) * cap, cap), cap)
            dst[me // per_block, mine, :] = src[h, me // per_block, mine, :]
            return copies

        going = []
        for h in range(halves):
            halo_copies[2 * h].wait_recv()
            halo_copies[2 * h + 1].wait_recv()
            sub = mid[h] + mm(qt[:, 0:rim], halo[0, h], NT) + mm(qt[:, rim + columns:], halo[1, h], NT)
            out_t[h] = sub.astype(BF16).reshape(blocks, block_points, half)
            going.append(exchange(h, out_t, g_t[h], go_send, go_recv))

        loads[6].wait()
        loads[7].wait()
        for j in range(blocks):
            for c in range(bands):
                wt[j, :, c * block_points:(c + 1) * block_points] = wb[j, c].T

        coming = []
        for h in range(halves):
            for copy in going[h]:
                copy.wait_recv()
            sums = [None] * blocks
            for j in range(blocks):
                sources = [lax.rem(sh[j, c] + j, blocks) for c in range(bands)]
                picked = jnp.concatenate([g_t[h][s] for s in sources], axis=0)
                forward = mm(wt[j], picked).astype(BF16)
                for c in range(bands):
                    term = mm(wb[j, c], forward)
                    for s in range(blocks):
                        part = term * (sources[c] == s).astype(F32)
                        sums[s] = part if sums[s] is None else sums[s] + part
            for s in range(blocks):
                adj_t[h, s] = sums[s].astype(BF16)
            coming.append(exchange(h, adj_t, inc[h], back_send, back_recv))

        edge_copies = []
        for h in range(halves):
            for copy in coming[h]:
                copy.wait_recv()
            came = inc_t[h].reshape(slots, half).T
            edge_out[0, h] = mm(came, qt[:, rim + columns:]).astype(BF16)
            edge_out[1, h] = mm(came, qt[:, 0:rim]).astype(BF16)
            for side, target in ((0, right_id), (1, left_id)):
                copy = pltpu.make_async_remote_copy(
                    src_ref=edge_out.at[side, h], dst_ref=edge_in.at[side, h],
                    send_sem=edge_send.at[side, h], recv_sem=edge_recv.at[side, h],
                    device_id=target, device_id_type=MESH,
                )
                copy.start()
                edge_copies.append(copy)
            out[h * half:(h + 1) * half, :] = mm(came, qt[:, rim:rim + columns])
        for h in range(halves):
            span = slice(h * half, (h + 1) * half)
            edge_copies[2 * h].wait_recv()
            edge_copies[2 * h + 1].wait_recv()
            out[span, 0:rim] += mm(edge_in[0, h], pick_left, NT)
            out[span, columns - rim:columns] += mm(edge_in[1, h], pick_right, NT)
        for copy in halo_copies + sum(going, []) + sum(coming, []) + edge_copies:
            copy.wait_send()

    return kernel


def solution(mesh):
    n_tile, n_conv = mesh.shape["tile"], mesh.shape["conv"]

    def on_device(field, interp, conv_blocks, band_shift, owner, edge_index):
        rows, columns = field.shape
        rim = edge_index.shape[1]
        extended, points = interp.shape
        blocks, bands, block_points, _ = conv_blocks.shape
        slots = blocks * block_points
        half, halves = 128, rows // 128
        body = make_kernel(n_tile, n_conv, rows, columns, rim, points, blocks, bands, block_points)
        sides = (2, halves, half, rim)
        cells = (halves, blocks, block_points, half)
        operands = [
            pltpu.with_memory_space_constraint(x, pltpu.HBM)
            for x in (field, interp, conv_blocks, band_shift, owner.reshape(1, points), edge_index)
        ]
        return pl.pallas_call(
            body,
            out_shape=jax.ShapeDtypeStruct((rows, columns), F32),
            in_specs=[pl.BlockSpec(memory_space=pltpu.HBM)] * 6,
            out_specs=pl.BlockSpec(memory_space=pltpu.VMEM),
            scratch_shapes=[
                pltpu.VMEM((rows, columns), F32),
                pltpu.VMEM((extended, points), BF16),
                pltpu.VMEM((blocks, bands, block_points, block_points), BF16),
                pltpu.SMEM((blocks, bands), jnp.int32),
                pltpu.VMEM((1, points), jnp.int32),
                pltpu.VMEM((2, rim), jnp.int32),
                pltpu.VMEM(sides, BF16),
                pltpu.VMEM(sides, BF16),
                pltpu.VMEM((slots, points), BF16),
                pltpu.VMEM((slots, extended), BF16),
                pltpu.VMEM((rows, columns), BF16),
                pltpu.VMEM((halves, slots, half), F32),
                pltpu.VMEM(cells, BF16),
                pltpu.VMEM(cells[1:], BF16),
                pltpu.VMEM(cells[1:], BF16),
                pltpu.VMEM(cells, BF16),
                pltpu.VMEM(cells, BF16),
                pltpu.VMEM(sides, BF16),
                pltpu.VMEM(sides, BF16),
                pltpu.VMEM((blocks, block_points, bands * block_points), BF16),
                pltpu.SemaphoreType.DMA((8,)),
                pltpu.SemaphoreType.DMA((2, halves)),
                pltpu.SemaphoreType.DMA((2, halves)),
                pltpu.SemaphoreType.DMA((halves, n_conv)),
                pltpu.SemaphoreType.DMA((halves, n_conv)),
                pltpu.SemaphoreType.DMA((halves, n_conv)),
                pltpu.SemaphoreType.DMA((halves, n_conv)),
                pltpu.SemaphoreType.DMA((2, halves)),
                pltpu.SemaphoreType.DMA((2, halves)),
            ],
            compiler_params=pltpu.CompilerParams(
                collective_id=0, has_side_effects=True, vmem_limit_bytes=24 * 1024 * 1024
            ),
        )(*operands)

    return jax.shard_map(
        on_device,
        mesh=mesh,
        in_specs=(
            P(None, ("tile", "conv")),
            P(("tile", "conv"), None),
            P(("tile", "conv"), None, None, None),
            P(("tile", "conv"), None),
            P(("tile", "conv"), None),
            P(("tile", "conv"), None),
        ),
        out_specs=P(None, ("tile", "conv")),
        check_vma=False,
    )
```

time: 81.9 us -> 46.5 us (0.57)
  Pallas kernels: 0 us -> 45.4 us
  starting transfers between devices: 37.3 us -> 0 us
  waiting for transfers between devices: 25.4 us -> 0 us
  matrix products: 6.94 us -> 0 us
  local copies, waits for them, and re-layouts: 6.3 us -> 0.88 us
  other arithmetic: 5.27 us -> 0 us
    pallas_call x0 -> x1, Pallas kernels: none -> 45.4 us  [on_device(): pl.pallas_call(body, out_shape=jax.ShapeDtypeStruct((rows, columns), F32)...]
    all_to_all x2 -> x0, waiting for transfers between devices: 22.6 us -> none  [the longest x1 11.7 us: on_device(): lax.all_to_all(outgoing, 'conv', split_axis=1, concat_axis=1, tiled=True)]
    ppermute x4 -> x0, starting transfers between devices: 22.3 us -> none  [the longest x1 13.2 us: padded(): lax.ppermute(head, axis, [((i + 1) % count, i) for i in range(count)])]
    all_to_all x2 -> x0, starting transfers between devices: 15 us -> none  [the longest x1 11.6 us: on_device(): lax.all_to_all(outgoing, 'conv', split_axis=1, concat_axis=1, tiled=True)]
    dot_general x10 -> x0, matrix products: 6.94 us -> none  [the longest x1 2.94 us: convolve(): jnp.einsum('rjbp,jbs->rsp', backward, select.astype(jnp.float32), precisi...]
    scatter-add x2 -> x0, other arithmetic: 3.19 us -> none  [the longest x1 1.6 us: on_device(): result = result.at[:, right_list].add(edge_sums[:, 3 * rim_width:])]
    ppermute x4 -> x0, waiting for transfers between devices: 2.77 us -> none  [the longest x1 2.76 us: with_halo(): lax.ppermute(leading, axis, [(b, a) for a, b in up])]
    convert_element_type x2 -> x0, local copies, waits for them, and re-layouts: 1.72 us -> none  [the longest x1 0.88 us: convolve(): return adjoint.reshape(height, owned_blocks * points).astype(jnp.bfloat16)]
  transfers between devices with their start and end apart: 6 -> 0, of which waited for: 3 -> 0; matrix products, arithmetic and copies ran while one was open for 4% -> 0% of each run, Pallas kernels for 0% -> 0%
where the time goes in v1:
time: 46.5 us; the launch traced here: 46.3 us
  Pallas kernels  45.4 us (98%)
  local copies, waits for them, and re-layouts  0.88 us (2%)
    pallas_call x1, Pallas kernels, on_device(): pl.pallas_call(body, out_shape=jax.ShapeDtypeStruct((rows, columns), F32)...  45.4 us

profile of v1, /device:TPU:1, one launch (start us, length us, event | category | flops | bytes accessed | tf_op | source)
XLA Modules:
  0.0 46.3 jit_solution(7060377041939266035)
XLA Ops:
  0.0 45.4 %shard_map.64 = f32[256,768]{1,0:T(8,128)S(1)} custom-call(f32[256,768]{1,0:T(8,128)} %field.1, bf16[1024,384]{1,0:T(8,128)(2,1)} %interp.1, bf16[2,3,256,256]{3,2,1,0:T(8,128)(2,1)} %conv.1, s32[2,3]{1,0:T(2,128)} %shift.1, s32[1,384]{1,0:T(1,128)} %bitcast.1, s32[2,128]{1,0:T(2,128)} %edges.1), custom_call_target="tpu_custom_call" | custom-call | tf_op jit(solution)/shard_map/pallas_call | solution.py:202
  45.4 0.9 %copy.8 = f32[256,768]{1,0:T(8,128)} copy(f32[256,768]{1,0:T(8,128)S(1)} %shard_map.64) | data formatting | bytes 1572864

commit v2 on v1

--- a/solution.py
+++ b/solution.py
@@ -16,10 +16,16 @@
     return lax.dot_general(a, b, dims, preferred_element_type=F32)
 
 
+def choose(pieces, source):
+    chosen = pieces[0]
+    for s in range(1, len(pieces)):
+        chosen = jnp.where(source == s, pieces[s], chosen)
+    return chosen
+
+
 def make_kernel(n_tile, n_conv, rows, columns, rim, points, blocks, bands, block_points):
     slots = blocks * block_points
     cap = slots // n_conv
-    per_block = block_points // cap
     half = 128
     halves = rows // half
     offsets = sorted(range(1, n_conv), key=lambda d: (-min(d, n_conv - d), d))
@@ -28,6 +34,7 @@
         field, interp, conv, shift, owner, edges, out,
         xf, ib, wb, sh, ow, eg, rims, halo, pt, qt, xb, mid, out_t, g_t0, g_t1, adj_t, inc_t, edge_out, edge_in, wt,
         load_sem, halo_send, halo_recv, go_send, go_recv, back_send, back_recv, edge_send, edge_recv,
+        near, up, down_sem,
     ):
         tile = lax.axis_index("tile")
         me = lax.axis_index("conv")
@@ -40,10 +47,6 @@
 
         def peer(d):
             return (tile, lax.rem(me + d, n_conv))
-
-        barrier = pltpu.get_barrier_semaphore()
-        for target in [left_id, right_id] + [peer(d) for d in offsets]:
-            pl.semaphore_signal(barrier, inc=1, device_id=target, device_id_type=MESH)
 
         loads = [
             pltpu.make_async_copy(edges, eg, load_sem.at[0]),
@@ -60,6 +63,16 @@
         for load in loads:
             load.start()
 
+        def tell(semaphore, target):
+            pl.semaphore_signal(semaphore, inc=1, device_id=target, device_id_type=MESH)
+
+        barrier = pltpu.get_barrier_semaphore()
+        tell(barrier, peer(n_conv - 1))
+        tell(barrier, left_id)
+        pl.semaphore_wait(barrier, 2)
+        tell(near.at[0], peer(1))
+        tell(near.at[1], right_id)
+
         for i in range(3):
             loads[i].wait()
         down = lax.broadcasted_iota(jnp.int32, (rim, rim), 0)
@@ -71,18 +84,31 @@
             xb[:, edge_cols[side]] = cells
             rims[side] = mm(cells, pick).astype(BF16).reshape(halves, half, rim)
 
-        pl.semaphore_wait(barrier, n_conv + 1)
-
-        halo_copies = []
-        for h in range(halves):
-            for side, target in ((0, right_id), (1, left_id)):
-                copy = pltpu.make_async_remote_copy(
-                    src_ref=rims.at[side, h], dst_ref=halo.at[side, h],
-                    send_sem=halo_send.at[side, h], recv_sem=halo_recv.at[side, h],
-                    device_id=target, device_id_type=MESH,
-                )
-                copy.start()
-                halo_copies.append(copy)
+        def halo_copy(side, h):
+            return pltpu.make_async_remote_copy(
+                src_ref=rims.at[side, h], dst_ref=halo.at[side, h],
+                send_sem=halo_send.at[side], recv_sem=halo_recv.at[side, h],
+                device_id=(right_id, left_id)[side], device_id_type=MESH,
+            )
+
+        for h in range(halves):
+            halo_copy(0, h).start()
+        pl.semaphore_wait(near.at[0], 1)
+        tell(up.at[0], peer(1))
+        tell(down_sem.at[0], peer(n_conv - 1))
+
+        @pl.when(me > 0)
+        def _():
+            pl.semaphore_wait(near.at[1], 1)
+            for h in range(halves):
+                halo_copy(1, h).start()
+
+        def widen(step, reach):
+            pl.semaphore_wait(up.at[step], 1)
+            pl.semaphore_wait(down_sem.at[step], 1)
+            if reach < n_conv // 2:
+                tell(up.at[step + 1], peer(reach))
+                tell(down_sem.at[step + 1], peer(n_conv - reach))
 
         loads[3].wait()
         owners = ow[...]
@@ -94,41 +120,55 @@
         rank = jnp.sum(before * named, axis=0, keepdims=True)
         slot = owners.astype(F32) * cap + rank
         pt[...] = (lax.broadcasted_iota(jnp.int32, (slots, points), 0).astype(F32) == slot).astype(F32).astype(BF16)
+        widen(0, 2)
         loads[4].wait()
         extended = columns + 2 * rim
         for start in range(0, extended, 256):
+            if start == 512:
+                widen(1, 4)
             qt[:, start:start + 256] = mm(pt[...], ib[start:start + 256, :], NT).astype(BF16)
         loads[5].wait()
         xb[:, rim:columns - rim] = xf[:, rim:columns - rim].astype(BF16)
         for h in range(halves):
             mid[h] = mm(qt[:, rim:rim + columns], xb[h * half:(h + 1) * half, :], NT)
 
+        widen(2, 8)
+
+        @pl.when(me == 0)
+        def _():
+            pl.semaphore_wait(near.at[1], 1)
+            for h in range(halves):
+                halo_copy(1, h).start()
+
         g_t = (g_t0, g_t1)
         inc = (inc_t.at[0], inc_t.at[1])
 
         def exchange(h, src, dst, send, recv):
-            copies = []
+            mine = pl.ds(pl.multiple_of(me * cap, cap), cap)
             for d in offsets:
                 to = lax.rem(me + d, n_conv)
-                copy = pltpu.make_async_remote_copy(
-                    src_ref=src.at[h, to // per_block, pl.ds(pl.multiple_of(lax.rem(to, per_block) * cap, cap), cap)],
-                    dst_ref=dst.at[me // per_block, pl.ds(pl.multiple_of(lax.rem(me, per_block) * cap, cap), cap)],
-                    send_sem=send.at[h, d], recv_sem=recv.at[h, d],
+                pltpu.make_async_remote_copy(
+                    src_ref=src.at[h, pl.ds(pl.multiple_of(to * cap, cap), cap)],
+                    dst_ref=dst.at[mine],
+                    send_sem=send.at[h], recv_sem=recv.at[h],
                     device_id=peer(d), device_id_type=MESH,
-                )
-                copy.start()
-                copies.append(copy)
-            mine = pl.ds(pl.multiple_of(lax.rem(me, per_block) * cap, cap), cap)
-            dst[me // per_block, mine, :] = src[h, me // per_block, mine, :]
-            return copies
-
-        going = []
-        for h in range(halves):
-            halo_copies[2 * h].wait_recv()
-            halo_copies[2 * h + 1].wait_recv()
+                ).start()
+            dst[mine, :] = src[h, mine, :]
+
+        def exchanged(h, src, dst, send, recv):
+            others = pl.ds(0, slots - cap)
+            return pltpu.make_async_remote_copy(
+                src_ref=src.at[h, others], dst_ref=dst.at[others],
+                send_sem=send.at[h], recv_sem=recv.at[h],
+                device_id=peer(1), device_id_type=MESH,
+            )
+
+        for h in range(halves):
+            halo_copy(0, h).wait_recv()
+            halo_copy(1, h).wait_recv()
             sub = mid[h] + mm(qt[:, 0:rim], halo[0, h], NT) + mm(qt[:, rim + columns:], halo[1, h], NT)
-            out_t[h] = sub.astype(BF16).reshape(blocks, block_points, half)
-            going.append(exchange(h, out_t, g_t[h], go_send, go_recv))
+            out_t[h] = sub.astype(BF16)
+            exchange(h, out_t, g_t[h], go_send, go_recv)
 
         loads[6].wait()
         loads[7].wait()
@@ -136,14 +176,13 @@
             for c in range(bands):
                 wt[j, :, c * block_points:(c + 1) * block_points] = wb[j, c].T
 
-        coming = []
-        for h in range(halves):
-            for copy in going[h]:
-                copy.wait_recv()
+        for h in range(halves):
+            exchanged(h, out_t, g_t[h], go_send, go_recv).wait_recv()
+            pieces = [g_t[h][s * block_points:(s + 1) * block_points, :] for s in range(blocks)]
             sums = [None] * blocks
             for j in range(blocks):
                 sources = [lax.rem(sh[j, c] + j, blocks) for c in range(bands)]
-                picked = jnp.concatenate([g_t[h][s] for s in sources], axis=0)
+                picked = jnp.concatenate([choose(pieces, s) for s in sources], axis=0)
                 forward = mm(wt[j], picked).astype(BF16)
                 for c in range(bands):
                     term = mm(wb[j, c], forward)
@@ -151,20 +190,19 @@
                         part = term * (sources[c] == s).astype(F32)
                         sums[s] = part if sums[s] is None else sums[s] + part
             for s in range(blocks):
-                adj_t[h, s] = sums[s].astype(BF16)
-            coming.append(exchange(h, adj_t, inc[h], back_send, back_recv))
+                adj_t[h, s * block_points:(s + 1) * block_points] = sums[s].astype(BF16)
+            exchange(h, adj_t, inc[h], back_send, back_recv)
 
         edge_copies = []
         for h in range(halves):
-            for copy in coming[h]:
-                copy.wait_recv()
-            came = inc_t[h].reshape(slots, half).T
+            exchanged(h, adj_t, inc[h], back_send, back_recv).wait_recv()
+            came = inc_t[h].T
             edge_out[0, h] = mm(came, qt[:, rim + columns:]).astype(BF16)
             edge_out[1, h] = mm(came, qt[:, 0:rim]).astype(BF16)
             for side, target in ((0, right_id), (1, left_id)):
                 copy = pltpu.make_async_remote_copy(
                     src_ref=edge_out.at[side, h], dst_ref=edge_in.at[side, h],
-                    send_sem=edge_send.at[side, h], recv_sem=edge_recv.at[side, h],
+                    send_sem=edge_send.at[side], recv_sem=edge_recv.at[side, h],
                     device_id=target, device_id_type=MESH,
                 )
                 copy.start()
@@ -176,8 +214,15 @@
             edge_copies[2 * h + 1].wait_recv()
             out[span, 0:rim] += mm(edge_in[0, h], pick_left, NT)
             out[span, columns - rim:columns] += mm(edge_in[1, h], pick_right, NT)
-        for copy in halo_copies + sum(going, []) + sum(coming, []) + edge_copies:
-            copy.wait_send()
+        for side in range(2):
+            for src, dst, send, recv in ((rims, halo, halo_send, halo_recv), (edge_out, edge_in, edge_send, edge_recv)):
+                pltpu.make_async_remote_copy(
+                    src_ref=src.at[side], dst_ref=dst.at[side], send_sem=send.at[side], recv_sem=recv.at[side, 0],
+                    device_id=right_id, device_id_type=MESH,
+                ).wait_send()
+        for h in range(halves):
+            exchanged(h, out_t, g_t[h], go_send, go_recv).wait_send()
+            exchanged(h, adj_t, inc[h], back_send, back_recv).wait_send()
 
     return kernel
 
@@ -194,7 +239,7 @@
         half, halves = 128, rows // 128
         body = make_kernel(n_tile, n_conv, rows, columns, rim, points, blocks, bands, block_points)
         sides = (2, halves, half, rim)
-        cells = (halves, blocks, block_points, half)
+        cells = (halves, slots, half)
         operands = [
             pltpu.with_memory_space_constraint(x, pltpu.HBM)
             for x in (field, interp, conv_blocks, band_shift, owner.reshape(1, points), edge_index)
@@ -226,14 +271,17 @@
                 pltpu.VMEM(sides, BF16),
                 pltpu.VMEM((blocks, block_points, bands * block_points), BF16),
                 pltpu.SemaphoreType.DMA((8,)),
+                pltpu.SemaphoreType.DMA((2,)),
                 pltpu.SemaphoreType.DMA((2, halves)),
+                pltpu.SemaphoreType.DMA((halves,)),
+                pltpu.SemaphoreType.DMA((halves,)),
+                pltpu.SemaphoreType.DMA((halves,)),
+                pltpu.SemaphoreType.DMA((halves,)),
+                pltpu.SemaphoreType.DMA((2,)),
                 pltpu.SemaphoreType.DMA((2, halves)),
-                pltpu.SemaphoreType.DMA((halves, n_conv)),
-                pltpu.SemaphoreType.DMA((halves, n_conv)),
-                pltpu.SemaphoreType.DMA((halves, n_conv)),
-                pltpu.SemaphoreType.DMA((halves, n_conv)),
-                pltpu.SemaphoreType.DMA((2, halves)),
-                pltpu.SemaphoreType.DMA((2, halves)),
+                pltpu.SemaphoreType.REGULAR((2,)),
+                pltpu.SemaphoreType.REGULAR((3,)),
+                pltpu.SemaphoreType.REGULAR((3,)),
             ],
             compiler_params=pltpu.CompilerParams(
                 collective_id=0, has_side_effects=True, vmem_limit_bytes=24 * 1024 * 1024

time: 46.5 us -> 44.2 us (0.951)
  Pallas kernels: 45.4 us -> 43.1 us
    pallas_call x1, Pallas kernels: 45.4 us -> 43.1 us  [on_device(): pl.pallas_call(body, out_shape=jax.ShapeDtypeStruct((rows, columns), F32)...]
where the time goes in v2:
time: 44.2 us; the launch traced here: 44 us
  Pallas kernels  43.1 us (98%)
  local copies, waits for them, and re-layouts  0.88 us (2%)
    pallas_call x1, Pallas kernels, on_device(): pl.pallas_call(body, out_shape=jax.ShapeDtypeStruct((rows, columns), F32)...  43.1 us

profile of v2, /device:TPU:1, one launch (start us, length us, event | category | flops | bytes accessed | tf_op | source)
XLA Modules:
  0.0 44.0 jit_solution(8618569559965861668)
XLA Ops:
  0.0 43.1 %shard_map.64 = f32[256,768]{1,0:T(8,128)S(1)} custom-call(f32[256,768]{1,0:T(8,128)} %field.1, bf16[1024,384]{1,0:T(8,128)(2,1)} %interp.1, bf16[2,3,256,256]{3,2,1,0:T(8,128)(2,1)} %conv.1, s32[2,3]{1,0:T(2,128)} %shift.1, s32[1,384]{1,0:T(1,128)} %bitcast.1, s32[2,128]{1,0:T(2,128)} %edges.1), custom_call_target="tpu_custom_call" | custom-call | tf_op jit(solution)/shard_map/pallas_call | solution.py:247
  43.1 0.9 %copy.8 = f32[256,768]{1,0:T(8,128)} copy(f32[256,768]{1,0:T(8,128)S(1)} %shard_map.64) | data formatting | bytes 1572864

commit v3 on v2

--- a/solution.py
+++ b/solution.py
@@ -60,7 +60,7 @@
             pltpu.make_async_copy(conv, wb, load_sem.at[6]),
             pltpu.make_async_copy(shift, sh, load_sem.at[7]),
         ]
-        for load in loads:
+        for load in loads[:4]:
             load.start()
 
         def tell(semaphore, target):
@@ -73,16 +73,14 @@
         tell(near.at[0], peer(1))
         tell(near.at[1], right_id)
 
-        for i in range(3):
-            loads[i].wait()
+        loads[0].wait()
+        loads[1].wait()
+        for load in loads[4:]:
+            load.start()
         down = lax.broadcasted_iota(jnp.int32, (rim, rim), 0)
         pick_left = (down == eg[0:1, :]).astype(F32).astype(BF16)
         pick_right = (down + (columns - rim) == eg[1:2, :]).astype(F32).astype(BF16)
         edge_cols = (slice(columns - rim, columns), slice(0, rim))
-        for side, pick in ((0, pick_right), (1, pick_left)):
-            cells = xf[:, edge_cols[side]].astype(BF16)
-            xb[:, edge_cols[side]] = cells
-            rims[side] = mm(cells, pick).astype(BF16).reshape(halves, half, rim)
 
         def halo_copy(side, h):
             return pltpu.make_async_remote_copy(
@@ -91,8 +89,16 @@
                 device_id=(right_id, left_id)[side], device_id_type=MESH,
             )
 
+        def fill_rim(side, pick):
+            cells = xf[:, edge_cols[side]].astype(BF16)
+            rims[side] = mm(cells, pick).astype(BF16).reshape(halves, half, rim)
+            xb[:, edge_cols[side]] = cells
+
+        fill_rim(0, pick_right)
         for h in range(halves):
             halo_copy(0, h).start()
+        loads[2].wait()
+        fill_rim(1, pick_left)
         pl.semaphore_wait(near.at[0], 1)
         tell(up.at[0], peer(1))
         tell(down_sem.at[0], peer(n_conv - 1))

time: 44.2 us -> 44.1 us (level)
  no operation moved by 1% of the time
where the time goes in v3:
time: 44.1 us; the launch traced here: 44 us
  Pallas kernels  43.1 us (98%)
  local copies, waits for them, and re-layouts  0.88 us (2%)
    pallas_call x1, Pallas kernels, on_device(): pl.pallas_call(body, out_shape=jax.ShapeDtypeStruct((rows, columns), F32)...  43.1 us
    unnamed x1, local copies, waits for them, and re-layouts  0.88 us

profile of v3, /device:TPU:1, one launch (start us, length us, event | category | flops | bytes accessed | tf_op | source)
XLA Modules:
  0.0 44.0 jit_solution(9757007158761945287)
XLA Ops:
  0.0 43.1 %shard_map.64 = f32[256,768]{1,0:T(8,128)S(1)} custom-call(f32[256,768]{1,0:T(8,128)} %field.1, bf16[1024,384]{1,0:T(8,128)(2,1)} %interp.1, bf16[2,3,256,256]{3,2,1,0:T(8,128)(2,1)} %conv.1, s32[2,3]{1,0:T(2,128)} %shift.1, s32[1,384]{1,0:T(1,128)} %bitcast.1, s32[2,128]{1,0:T(2,128)} %edges.1), custom_call_target="tpu_custom_call" | custom-call | tf_op jit(solution)/shard_map/pallas_call | solution.py:253
  43.1 0.9 %copy.8 = f32[256,768]{1,0:T(8,128)} copy(f32[256,768]{1,0:T(8,128)S(1)} %shard_map.64) | data formatting | bytes 1572864

commit v4 on v3

--- a/solution.py
+++ b/solution.py
@@ -29,6 +29,8 @@
     half = 128
     halves = rows // half
     offsets = sorted(range(1, n_conv), key=lambda d: (-min(d, n_conv - d), d))
+
+    far = 9
 
     def kernel(
         field, interp, conv, shift, owner, edges, out,
@@ -149,9 +151,9 @@
         g_t = (g_t0, g_t1)
         inc = (inc_t.at[0], inc_t.at[1])
 
-        def exchange(h, src, dst, send, recv):
+        def exchange(h, src, dst, send, recv, steps):
             mine = pl.ds(pl.multiple_of(me * cap, cap), cap)
-            for d in offsets:
+            for d in steps:
                 to = lax.rem(me + d, n_conv)
                 pltpu.make_async_remote_copy(
                     src_ref=src.at[h, pl.ds(pl.multiple_of(to * cap, cap), cap)],
@@ -159,7 +161,8 @@
                     send_sem=send.at[h], recv_sem=recv.at[h],
                     device_id=peer(d), device_id_type=MESH,
                 ).start()
-            dst[mine, :] = src[h, mine, :]
+            if len(steps) > 1 and steps[0] == offsets[0]:
+                dst[mine, :] = src[h, mine, :]
 
         def exchanged(h, src, dst, send, recv):
             others = pl.ds(0, slots - cap)
@@ -174,7 +177,7 @@
             halo_copy(1, h).wait_recv()
             sub = mid[h] + mm(qt[:, 0:rim], halo[0, h], NT) + mm(qt[:, rim + columns:], halo[1, h], NT)
             out_t[h] = sub.astype(BF16)
-            exchange(h, out_t, g_t[h], go_send, go_recv)
+            exchange(h, out_t, g_t[h], go_send, go_recv, offsets)
 
         loads[6].wait()
         loads[7].wait()
@@ -197,7 +200,10 @@
                         sums[s] = part if sums[s] is None else sums[s] + part
             for s in range(blocks):
                 adj_t[h, s * block_points:(s + 1) * block_points] = sums[s].astype(BF16)
-            exchange(h, adj_t, inc[h], back_send, back_recv)
+            exchange(h, adj_t, inc[h], back_send, back_recv, offsets[:far])
+        for d in offsets[far:]:
+            for h in range(halves):
+                exchange(h, adj_t, inc[h], back_send, back_recv, [d])
 
         edge_copies = []
         for h in range(halves):

time: 44.1 us -> 44.1 us (level)
  no operation moved by 1% of the time
where the time goes in v4:
time: 44.1 us; the launch traced here: 43.9 us
  Pallas kernels  43 us (98%)
  local copies, waits for them, and re-layouts  0.88 us (2%)
    pallas_call x1, Pallas kernels, on_device(): pl.pallas_call(body, out_shape=jax.ShapeDtypeStruct((rows, columns), F32)...  43 us
    unnamed x1, local copies, waits for them, and re-layouts  0.88 us

profile of v4, /device:TPU:1, one launch (start us, length us, event | category | flops | bytes accessed | tf_op | source)
XLA Modules:
  0.0 43.9 jit_solution(8972595975167803250)
XLA Ops:
  0.0 43.0 %shard_map.64 = f32[256,768]{1,0:T(8,128)S(1)} custom-call(f32[256,768]{1,0:T(8,128)} %field.1, bf16[1024,384]{1,0:T(8,128)(2,1)} %interp.1, bf16[2,3,256,256]{3,2,1,0:T(8,128)(2,1)} %conv.1, s32[2,3]{1,0:T(2,128)} %shift.1, s32[1,384]{1,0:T(1,128)} %bitcast.1, s32[2,128]{1,0:T(2,128)} %edges.1), custom_call_target="tpu_custom_call" | custom-call | tf_op jit(solution)/shard_map/pallas_call | solution.py:259
  43.1 0.9 %copy.8 = f32[256,768]{1,0:T(8,128)} copy(f32[256,768]{1,0:T(8,128)S(1)} %shard_map.64) | data formatting | bytes 1572864
